TPU v7x, 32 devices: a whole 2x2x4 slice. The times are simulated.
32 devices in a mesh: cells: 8 (over z, y), bins: 4 (over x, core).
Axes of the slice: x: 2, y: 2, z: 4, core: 2. Of those that a mesh axis runs over, the one named last changes fastest.
Arguments:
- snapshots: bfloat16 [4, 65536, 512], P('bins', 'cells'), may hold values from -150 to 150
- training: int32 [65536], P('cells'), may hold values 0 or 1
- doppler: int32 [4, 128], P('bins'), may hold values from 0 to 1023
Outputs:
- filtered: bfloat16 [4, 256, 65536], P('bins', None, 'cells')
All inputs are finite; a program needn't handle non-finite values. No bound on the sum of `training` on one device may be relied on, other than what follows from the above.
Results may differ from a plain program's by a relative error of at most 0.003.
The roundings to bfloat16 on the way count: a program that leaves them out, or rounds other values in their place, can miss the bound.
Values sent between devices are 32-bit elements; how exact they have to be, the bound alone decides.
A program may use at most 64 MiB of HBM per device.

v0:
```python
import jax
import jax.numpy as jnp
from jax import lax
from jax.sharding import PartitionSpec as P

CHANNELS = 16
PULSES = 16
NDOPP = 1024


load_ratio = 0.5
look_freq = 0.125


def steering(doppler, chans, pulses):
    index = jnp.arange(chans * pulses)
    chan = (index // pulses).astype(jnp.float32)
    pulse = (index % pulses).astype(jnp.float32)
    freq = doppler.astype(jnp.float32) / NDOPP - 0.5
    phase = 2.0 * jnp.pi * (look_freq * chan[:, None] + pulse[:, None] * freq[None, :])
    return jnp.concatenate([jnp.cos(phase), jnp.sin(phase)], 0) / jnp.sqrt(
        jnp.float32(chans * pulses)
    )


def complex_parts(gram):
    half = gram.shape[0] // 2
    upper = gram[:half, :half]
    cross = gram[:half, half:]
    lower = gram[half:, half:]
    return (upper + lower, cross.T - cross)


def per_device(snapshots, training, doppler):
    snaps = snapshots[0]
    keep = training.astype(jnp.bfloat16)[:, None]
    gram = lax.dot_general(
        snaps * keep, snaps, (((0,), (0,)), ((), ())), preferred_element_type=jnp.float32
    )
    half = snaps.shape[1] // 2
    local_real, local_imag = complex_parts(gram)
    rows = jnp.arange(half)[:, None]
    cols = jnp.arange(half)[None, :]
    upper_side = rows <= cols
    packed = jnp.where(upper_side, local_real, local_imag)
    summed = lax.psum(packed, "cells")
    real_part = jnp.where(upper_side, summed, summed.T)
    imag_part = jnp.where(
        rows > cols, summed, jnp.where(rows < cols, -summed.T, jnp.zeros_like(summed))
    )
    power = lax.psum(jnp.trace(real_part), "bins")
    noise = power / (lax.axis_size("bins") * half)
    loaded = real_part + load_ratio * noise * jnp.eye(half, dtype=jnp.float32)
    embed = jnp.concatenate(
        [jnp.concatenate([loaded, -imag_part], 1), jnp.concatenate([imag_part, loaded], 1)], 0
    )
    factor = jnp.linalg.cholesky(embed)
    steer = steering(doppler[0], CHANNELS, PULSES)
    weights = jax.scipy.linalg.cho_solve((factor, True), steer)
    gain = jnp.sum(steer * weights, axis=0)
    w_real = weights[:half] / gain[None, :]
    w_imag = weights[half:] / gain[None, :]
    taps = jnp.concatenate(
        [jnp.concatenate([w_real, w_imag], 0), jnp.concatenate([-w_imag, w_real], 0)], 1
    ).astype(jnp.bfloat16)
    result = lax.dot_general(
        taps, snaps, (((0,), (1,)), ((), ())), preferred_element_type=jnp.float32
    )
    return result.astype(jnp.bfloat16)[None]


def solution(mesh):
    in_specs = (P("bins", "cells", None), P("cells"), P("bins", None))
    out_specs = P("bins", None, "cells")
    return jax.shard_map(
        per_device, mesh=mesh, in_specs=in_specs, out_specs=out_specs, check_vma=False
    )
```

profile of v0, /device:TPU:0, one launch (start us, length us, event | category | flops | bytes accessed | tf_op | source)
XLA Modules:
  0.0 257.7 jit_solution(10029392906276023549)
XLA Ops:
  6.5 0.8 convert_element_type.26
  7.3 10.5 %fusion.2 = f32[512,512]{1,0:T(8,128)S(1)} fusion(bf16[1,8192,512]{2,1,0:T(8,128)(2,1)} %param.3, bf16[8192]{0:T(1024)(128)(2,1)S(1)} %convert_element_type.26), kind=kOutput, calls=%fused_computation.5 | convolution fusion | flops 4299161600 | bytes 9453568 | tf_op jit(solution)/shard_map/dot_general | solution.py:37
  18.0 0.8 fusion.9
  18.8 0.6 fusion.44
  19.6 73.0 %all-reduce.3.cloned.1.call-done = f32[256,256]{1,0:T(8,128)} async-done(((f32[256,256]{1,0:T(8,128)}), f32[256,256]{1,0:T(8,128)}) %all-reduce.3.cloned.1.call-update) | async-done | bytes 262160 | tf_op jit(solution)/shard_map/psum | solution.py:46
  92.6 1.1 copy.6
  93.7 1.7 select_reduce_fusion
  95.4 6.3 %psum.15 = f32[]{:T(128)} all-reduce(f32[]{:T(128)} %select_reduce_fusion), channel_id=1, replica_groups=mesh['cells'=8,'bins'=4] {'bins'}, use_global_device_ids=true, to_apply=%region_2.3 | all-reduce | flops 1 | bytes 8 | tf_op jit(solution)/shard_map/psum | solution.py:51
  102.4 1.0 fusion.73
  104.1 11.7 %cholesky.104 = f32[128,128]{1,0:T(8,128)S(1)} custom-call(f32[128,128]{1,0:T(8,128)S(1)} %cholesky.266), custom_call_target="Cholesky" | custom-call | tf_op jit(solution)/shard_map/jit(cholesky)/cholesky | solution.py:57
  115.8 9.8 %custom-call.34 = f32[1,128,128]{1,2,0:T(8,128)S(1)} custom-call(f32[1,128,128]{2,1,0:T(8,128)S(1)} %get-tuple-element.37), custom_call_target="InvertDiagBlocksLowerTriangular" | custom-call | tf_op jit(solution)/shard_map/jit(cholesky)/cholesky | solution.py:57
  126.5 11.7 %cholesky.217 = f32[128,128]{1,0:T(8,128)S(1)} custom-call(f32[128,128]{1,0:T(8,128)S(1)} %cholesky.270), custom_call_target="Cholesky" | custom-call | tf_op jit(solution)/shard_map/jit(cholesky)/cholesky | solution.py:57
  138.2 10.0 %custom-call.35 = f32[1,128,128]{1,2,0:T(8,128)S(1)} custom-call(f32[1,128,128]{2,1,0:T(8,128)S(1)} %get-tuple-element.34), custom_call_target="InvertDiagBlocksLowerTriangular" | custom-call | tf_op jit(solution)/shard_map/jit(cholesky)/cholesky | solution.py:57
  148.9 11.7 %cholesky.238 = f32[128,128]{1,0:T(8,128)S(1)} custom-call(f32[128,128]{1,0:T(8,128)S(1)} %cholesky.275), custom_call_target="Cholesky" | custom-call | tf_op jit(solution)/shard_map/jit(cholesky)/cholesky | solution.py:57
  160.6 0.7 compare_reduce_fusion.1
  161.3 9.8 %custom-call.36 = f32[1,128,128]{1,2,0:T(8,128)S(1)} custom-call(f32[1,128,128]{2,1,0:T(8,128)S(1)} %get-tuple-element.31), custom_call_target="InvertDiagBlocksLowerTriangular" | custom-call | tf_op jit(solution)/shard_map/jit(cholesky)/cholesky | solution.py:57
  171.7 11.7 %cholesky.255 = f32[128,128]{1,0:T(8,128)S(1)} custom-call(f32[128,128]{1,0:T(8,128)S(1)} %convolution_subtract_fusion.8), custom_call_target="Cholesky" | custom-call | tf_op jit(solution)/shard_map/jit(cholesky)/cholesky | solution.py:57
  183.5 0.7 compare_reduce_fusion
  184.2 0.7 compare_reduce_fusion.2
  187.8 10.5 %while.1 = (s32[]{:T(128)}, f32[512,512]{1,0:T(8,128)S(1)}, s32[4,2]{0,1:T(2,128)S(1)}, f32[4,128,128]{2,1,0:T(8,128)}, s32[]{:T(128)}) while((s32[]{:T(128)}, f32[512,512]{1,0:T(8,128)S(1)}, s32[4,2]{0,1:T(2,128)S(1)}, f32[4,128,128]{2,1,0:T(8,128)}, s32[]{:T(128)}) %tuple.32), condition=%wide.while_cond, body=%wide.while_body.sunk | while | flops 2 | bytes 132205 | solution.py:59
  187.8 0.6 fusion.87
  188.4 2.0 bitcast_dynamic-update-slice_fusion.2
  190.5 0.6 fusion.87
  191.1 2.0 bitcast_dynamic-update-slice_fusion.2
  193.1 0.6 fusion.87
  193.7 2.0 bitcast_dynamic-update-slice_fusion.2
  195.7 0.6 fusion.87
  196.3 2.0 bitcast_dynamic-update-slice_fusion.2
  198.3 40.1 %custom-call.37 = f32[4,128,128]{1,2,0:T(8,128)S(1)} custom-call(f32[4,128,128]{2,1,0:T(8,128)} %get-tuple-element.12), custom_call_target="InvertDiagBlocksLowerTriangular" | custom-call | tf_op jit(solution)/shard_map/jit(_cho_solve)/triangular_solve | solution.py:59
  241.1 0.4 convolution_subtract_fusion.2
  241.7 0.5 convolution_subtract_fusion.6
  242.5 7.9 %fusion = bf16[1,256,8192]{2,1,0:T(8,128)(2,1)} fusion(bf16[1,8192,512]{2,1,0:T(8,128)(2,1)} %param.3, bf16[256,128]{1,0:T(8,128)(2,1)S(1)} %get-tuple-element.40, bf16[256,128]{1,0:T(8,128)(2,1)S(1)} %get-tuple-element.27, bf16[256,128]{1,0:T(8,128)(2,1)S(1)} %get-tuple-element.26), kind=kOutput, calls=%fused_computation.3 | convolution fusion | flops 2150629376 | bytes 12779520 | tf_op jit(solution)/shard_map/dot_general | solution.py:66
  (51 shorter events, 7.0 us)
Async XLA Ops:
  6.5 86.1 %all-reduce.3.cloned.1.call-start = ((), (), s32[]{:S(2)}) async-start(), calls=%async_computation | async-start | bytes 524288 | tf_op jit(solution)/shard_map/psum | solution.py:46
  7.3 11.5 %copy-start = (s32[1,128]{1,0:T(1,128)S(1)}, s32[1,128]{1,0:T(1,128)}, u32[]{:S(2)}) copy-start(s32[1,128]{1,0:T(1,128)} %param.5) | copy-start | bytes 1540
Sparse Core Ops, SparseCore 0:
  18.9 73.6 all-reduce.2
where the time goes:
time: 262 us; the launch traced here: 258 us
  other arithmetic  124 us (47%)
  waiting for transfers between devices  73 us (28%)
  matrix products  24.2 us (9%)
  between operations  17.4 us (7%)
  local copies, waits for them, and re-layouts  12.4 us (5%)
  blocking collectives  6.35 us (2%)
    another operation x14, other arithmetic, per_device(): factor = jnp.linalg.cholesky(embed)  78.7 us
    psum x1, waiting for transfers between devices, per_device(): summed = lax.psum(packed, 'cells')  73 us
    another operation x3, other arithmetic, per_device(): weights = jax.scipy.linalg.cho_solve((factor, True), steer)  40.5 us
    dot_general x1, matrix products, per_device(): lax.dot_general(snaps * keep, snaps, (((0,), (0,)), ((), ())), preferred_...  10.5 us
    another operation x12, local copies, waits for them, and re-layouts  10.5 us
    dot_general x1, matrix products, per_device(): lax.dot_general(taps, snaps, (((0,), (1,)), ((), ())), preferred_element_...  7.91 us
    psum x1, blocking collectives, per_device(): power = lax.psum(jnp.trace(real_part), 'bins')  6.35 us
  transfers between devices with their start and end apart: 1, of which 1 were waited for; matrix products, arithmetic and copies ran while one was open for 0% of the time, Pallas kernels for 0%

commit v1 on v0

v1 whole, which is shorter than its diff:
```python
import functools

import jax
import jax.numpy as jnp
from jax import lax
from jax.experimental import pallas as pl
from jax.experimental.pallas import tpu as pltpu
from jax.sharding import PartitionSpec as P

CHANNELS = 16
PULSES = 16
NDOPP = 1024


load_ratio = 0.5
look_freq = 0.125

EXTRA = 8
DONE = 0.99
REFINE = 2
HIGH = lax.Precision.HIGH
HIGHEST = lax.Precision.HIGHEST
MESH = pl.DeviceIdType.MESH


def steering(doppler, chans, pulses):
    index = jnp.arange(chans * pulses)
    chan = (index // pulses).astype(jnp.float32)
    pulse = (index % pulses).astype(jnp.float32)
    freq = doppler.astype(jnp.float32) / NDOPP - 0.5
    phase = 2.0 * jnp.pi * (look_freq * chan[:, None] + pulse[:, None] * freq[None, :])
    return jnp.concatenate([jnp.cos(phase), jnp.sin(phase)], 0) / jnp.sqrt(
        jnp.float32(chans * pulses)
    )


def gram_kernel(half, x_ref, keep_ref, out_ref, real_sum, cross_sum):
    step = pl.program_id(0)

    @pl.when(step == 0)
    def _():
        real_sum[...] = jnp.zeros_like(real_sum)
        cross_sum[...] = jnp.zeros_like(cross_sum)

    x = x_ref[...]
    keep = keep_ref[...].astype(jnp.bfloat16)
    masked = x.T * keep
    mr, mi = masked[:half], masked[half:]
    r, i = x[:, :half], x[:, half:]
    real_sum[...] += jnp.dot(
        jnp.concatenate([mr, mi], 1),
        jnp.concatenate([r, i], 0),
        preferred_element_type=jnp.float32,
    )
    cross_sum[...] += jnp.dot(mr, i, preferred_element_type=jnp.float32)

    @pl.when(step == pl.num_programs(0) - 1)
    def _():
        real = real_sum[...]
        cross = cross_sum[...]
        rows = lax.broadcasted_iota(jnp.int32, (half, half), 0)
        cols = lax.broadcasted_iota(jnp.int32, (half, half), 1)
        out_ref[...] = jnp.where(rows <= cols, real, cross.T - cross)


def gram(snaps, keep, block):
    cells, width = snaps.shape
    half = width // 2
    return pl.pallas_call(
        functools.partial(gram_kernel, half),
        grid=(cells // block,),
        in_specs=[
            pl.BlockSpec((block, width), lambda i: (i, 0)),
            pl.BlockSpec((1, block), lambda i: (0, i)),
        ],
        out_specs=pl.BlockSpec((half, half), lambda i: (0, 0)),
        out_shape=jax.ShapeDtypeStruct((half, half), jnp.float32),
        scratch_shapes=[
            pltpu.VMEM((half, half), jnp.float32),
            pltpu.VMEM((half, half), jnp.float32),
        ],
        name="gram",
    )(snaps, keep)


def sum_kernel(n, m, x_ref, out_ref, rs_buf, tr_src, tr_buf, mine, sems):
    me = lax.axis_index("cells")
    g = lax.axis_index("bins")
    half = x_ref.shape[0]
    rows = half // n
    rs_send, rs_recv, tr_send, tr_recv, ag_send, ag_recv = sems

    barrier = pltpu.get_barrier_semaphore()
    for k in range(1, n):
        pl.semaphore_signal(
            barrier, inc=1, device_id=(lax.rem(me + k, n), g), device_id_type=MESH
        )
    for k in range(1, m):
        pl.semaphore_signal(
            barrier, inc=1, device_id=(me, lax.rem(g + k, m)), device_id_type=MESH
        )
    pl.semaphore_wait(barrier, n + m - 2)

    copies = []
    for k in range(1, n):
        peer = lax.rem(me + k, n)
        copy = pltpu.make_async_remote_copy(
            src_ref=x_ref.at[pl.ds(pl.multiple_of(peer * rows, rows), rows)],
            dst_ref=rs_buf.at[k - 1],
            send_sem=rs_send.at[k - 1],
            recv_sem=rs_recv.at[k - 1],
            device_id=(peer, g),
            device_id_type=MESH,
        )
        copy.start()
        copies.append(copy)
    r = lax.broadcasted_iota(jnp.int32, (half, half), 0)
    c = lax.broadcasted_iota(jnp.int32, (half, half), 1)
    trace = jnp.sum(jnp.where(r == c, x_ref[...], 0.0), axis=0, keepdims=True)
    tr_src[...] = jnp.broadcast_to(trace, tr_src.shape)
    for k in range(1, m):
        copy = pltpu.make_async_remote_copy(
            src_ref=tr_src,
            dst_ref=tr_buf.at[k - 1],
            send_sem=tr_send.at[k - 1],
            recv_sem=tr_recv.at[k - 1],
            device_id=(me, lax.rem(g + k, m)),
            device_id_type=MESH,
        )
        copy.start()
        copies.append(copy)
    for copy in copies:
        copy.wait()
    total = x_ref[pl.ds(pl.multiple_of(me * rows, rows), rows), :]
    for k in range(n - 1):
        total = total + rs_buf[k]
    power = tr_src[...]
    for k in range(m - 1):
        power = power + tr_buf[k]
    mine[pl.ds(0, rows), :] = total
    mine[pl.ds(rows, EXTRA), :] = power
    out_ref[me] = jnp.concatenate([total, power], 0)

    copies = []
    for k in range(1, n):
        copy = pltpu.make_async_remote_copy(
            src_ref=mine,
            dst_ref=out_ref.at[me],
            send_sem=ag_send.at[k - 1],
            recv_sem=ag_recv.at[k - 1],
            device_id=(lax.rem(me + k, n), g),
            device_id_type=MESH,
        )
        copy.start()
        copies.append(copy)
    for k in range(1, n):
        copies[k - 1].wait_send()
        pltpu.make_async_remote_copy(
            src_ref=mine,
            dst_ref=out_ref.at[lax.rem(me + n - k, n)],
            send_sem=ag_send.at[k - 1],
            recv_sem=ag_recv.at[k - 1],
            device_id=(lax.rem(me + n - k, n), g),
            device_id_type=MESH,
        ).wait_recv()


def all_sum(packed):
    n, m = lax.axis_size("cells"), lax.axis_size("bins")
    half = packed.shape[0]
    rows = half // n
    dma = pltpu.SemaphoreType.DMA
    return pl.pallas_call(
        functools.partial(sum_kernel, n, m),
        out_shape=jax.ShapeDtypeStruct((n, rows + EXTRA, half), jnp.float32),
        in_specs=[pl.BlockSpec(memory_space=pltpu.VMEM)],
        out_specs=pl.BlockSpec(memory_space=pltpu.VMEM),
        scratch_shapes=[
            pltpu.VMEM((n - 1, rows, half), jnp.float32),
            pltpu.VMEM((EXTRA, half), jnp.float32),
            pltpu.VMEM((m - 1, EXTRA, half), jnp.float32),
            pltpu.VMEM((rows + EXTRA, half), jnp.float32),
            [dma((n - 1,)), dma((n - 1,)), dma((m - 1,)), dma((m - 1,)), dma((n - 1,)), dma((n - 1,))],
        ],
        compiler_params=pltpu.CompilerParams(collective_id=0, has_side_effects=True),
        name="all_sum",
    )(packed)


def newton_steps(ratio):
    d, steps = 1.0 / (ratio + 1.0), 0
    while d < DONE:
        d = (4.0 * d - 2.0 * d * d) / (1.0 + 2.0 * d - d * d)
        steps += 1
    return steps - 1


def solve_kernel(groups, parts_ref, steer_ref, taps_ref, mat, full, col):
    n = parts_ref.shape[0]
    rows = parts_ref.shape[1] - EXTRA
    half = parts_ref.shape[2]
    summed = jnp.concatenate([parts_ref[k, :rows, :] for k in range(n)], 0)
    power_row = parts_ref[0, rows:rows + 1, :]
    for k in range(1, n):
        power_row = power_row + parts_ref[k, rows:rows + 1, :]
    noise = jnp.sum(power_row, axis=1, keepdims=True) / (groups * half)
    low = load_ratio * noise
    r = lax.broadcasted_iota(jnp.int32, (half, half), 0)
    c = lax.broadcasted_iota(jnp.int32, (half, half), 1)
    flip = summed.T
    trace = jnp.sum(
        jnp.sum(jnp.where(r == c, summed, 0.0), axis=0, keepdims=True), axis=1, keepdims=True
    )
    eye = jnp.where(r == c, 1.0, 0.0)
    scale = 1.0 / (0.5 * trace + low)
    real = (jnp.where(r <= c, summed, flip) + low * eye) * scale
    imag = jnp.where(r > c, summed, jnp.where(r < c, -flip, 0.0)) * scale
    mat[:half, :half] = real
    mat[half:, half:] = real
    mat[:half, half:] = -imag
    mat[half:, :half] = imag

    def put(xr, xi):
        col[:half, :] = xr
        col[half:, :] = xi
        full[:half, :half] = xr
        full[half:, half:] = xr
        full[:half, half:] = -xi
        full[half:, :half] = xi

    d = low * scale
    bend = 2.0 / (1.0 + 2.0 * d - d * d)
    d = (4.0 * d - 2.0 * d * d) / (1.0 + 2.0 * d - d * d)
    put(bend * (2.0 * eye - real), -bend * imag)

    def newton(_, d):
        left = jnp.dot(mat[...], col[...], preferred_element_type=jnp.float32, precision=HIGH)
        bend = 2.0 / (1.0 + 2.0 * d - d * d)
        step = jnp.dot(
            full[...],
            jnp.concatenate([2.0 * eye - left[:half], -left[half:]], 0),
            preferred_element_type=jnp.float32,
            precision=HIGH,
        )
        put(bend * step[:half], bend * step[half:])
        return (4.0 * d - 2.0 * d * d) / (1.0 + 2.0 * d - d * d)

    lax.fori_loop(0, newton_steps(groups * half), newton, d)

    steer = steer_ref[...]
    w = jnp.dot(full[...], steer, preferred_element_type=jnp.float32, precision=HIGH)
    for _ in range(REFINE):
        gap = steer - jnp.dot(mat[...], w, preferred_element_type=jnp.float32, precision=HIGHEST)
        w = w + jnp.dot(full[...], gap, preferred_element_type=jnp.float32, precision=HIGH)
    w = w * scale
    gain = jnp.sum(steer * w, axis=0, keepdims=True)
    wr = (w[:half] / gain).T
    wi = (w[half:] / gain).T
    bins = wr.shape[0]
    taps_ref[:bins, :half] = wr.astype(jnp.bfloat16)
    taps_ref[:bins, half:] = wi.astype(jnp.bfloat16)
    taps_ref[bins:, :half] = (-wi).astype(jnp.bfloat16)
    taps_ref[bins:, half:] = wr.astype(jnp.bfloat16)


def solve(parts, steer, groups):
    half = parts.shape[2]
    bins = steer.shape[1]
    return pl.pallas_call(
        functools.partial(solve_kernel, groups),
        out_shape=jax.ShapeDtypeStruct((2 * bins, 2 * half), jnp.bfloat16),
        in_specs=[pl.BlockSpec(memory_space=pltpu.VMEM)] * 2,
        out_specs=pl.BlockSpec(memory_space=pltpu.VMEM),
        scratch_shapes=[
            pltpu.VMEM((2 * half, 2 * half), jnp.float32),
            pltpu.VMEM((2 * half, 2 * half), jnp.float32),
            pltpu.VMEM((2 * half, half), jnp.float32),
        ],
        name="solve",
    )(parts, steer)


def filter_kernel(taps_ref, x_ref, out_ref):
    out_ref[...] = lax.dot_general(
        taps_ref[...], x_ref[...], (((1,), (1,)), ((), ())), preferred_element_type=jnp.float32
    ).astype(out_ref.dtype)


def apply_taps(taps, snaps, block):
    cells, width = snaps.shape
    rows = taps.shape[0]
    return pl.pallas_call(
        filter_kernel,
        grid=(cells // block,),
        in_specs=[
            pl.BlockSpec((rows, width), lambda i: (0, 0)),
            pl.BlockSpec((block, width), lambda i: (i, 0)),
        ],
        out_specs=pl.BlockSpec((rows, block), lambda i: (0, i)),
        out_shape=jax.ShapeDtypeStruct((rows, cells), jnp.bfloat16),
        name="filter",
    )(taps, snaps)


def per_device(snapshots, training, doppler):
    snaps = snapshots[0]
    block = min(1024, snaps.shape[0])
    packed = gram(snaps, training[None, :], block)
    parts = all_sum(packed)
    steer = steering(doppler[0], CHANNELS, PULSES)
    taps = solve(parts, steer, lax.axis_size("bins"))
    return apply_taps(taps, snaps, block)[None]


def solution(mesh):
    in_specs = (P("bins", "cells", None), P("cells"), P("bins", None))
    out_specs = P("bins", None, "cells")
    return jax.shard_map(
        per_device, mesh=mesh, in_specs=in_specs, out_specs=out_specs, check_vma=False
    )
```

time: 262 us -> 60.3 us (0.23); the launches traced: 258 us -> 59.1 us
  other arithmetic: 124 us -> 1.97 us
  waiting for transfers between devices: 73 us -> 0 us
  Pallas kernels: 0 us -> 57.1 us
  matrix products: 24.2 us -> 0 us
  between operations: 17.4 us -> 0.02 us
  local copies, waits for them, and re-layouts: 12.4 us -> 0 us
  blocking collectives: 6.35 us -> 0 us
    another operation x18 -> x0, other arithmetic: 119 us -> none  [the longest x14 78.7 us: per_device(): factor = jnp.linalg.cholesky(embed)]
    psum x1 -> x0, waiting for transfers between devices: 73 us -> none  [per_device(): summed = lax.psum(packed, 'cells')]
    pallas_call x0 -> x4, Pallas kernels: none -> 57.1 us  [the longest x1 20.1 us: all_sum(): pl.pallas_call(functools.partial(sum_kernel, n, m), out_shape=jax.ShapeDt...]
    dot_general x2 -> x0, matrix products: 18.4 us -> none  [the longest x1 10.5 us: per_device(): lax.dot_general(snaps * keep, snaps, (((0,), (0,)), ((), ())), preferred_...]
    another operation x17 -> x0, local copies, waits for them, and re-layouts: 10.6 us -> none
    psum x1 -> x0, blocking collectives: 6.35 us -> none  [per_device(): power = lax.psum(jnp.trace(real_part), 'bins')]
    another operation x20 -> x0, matrix products: 5.79 us -> none  [the longest x14 3.91 us: per_device(): weights = jax.scipy.linalg.cho_solve((factor, True), steer)]
  transfers between devices with their start and end apart: 1 -> 0, of which waited for: 1 -> 0; matrix products, arithmetic and copies ran while one was open for 0% -> 0% of each run, Pallas kernels for 0% -> 0%
where the time goes in v1:
time: 60.3 us; the launch traced here: 59.1 us
  Pallas kernels  57.1 us (95%)
  other arithmetic  1.97 us (3%)
    pallas_call x1, Pallas kernels, all_sum(): pl.pallas_call(functools.partial(sum_kernel, n, m), out_shape=jax.ShapeDt...  20.1 us
    pallas_call x1, Pallas kernels, solve(): pl.pallas_call(functools.partial(solve_kernel, groups), out_shape=jax.Sha...  18.8 us
    pallas_call x1, Pallas kernels, gram(): pl.pallas_call(functools.partial(gram_kernel, half), grid=(cells // block...  9.16 us
    pallas_call x1, Pallas kernels, apply_taps(): pl.pallas_call(filter_kernel, grid=(cells // block,), in_specs=[pl.BlockS...  9.03 us

profile of v1, /device:TPU:0, one launch (start us, length us, event | category | flops | bytes accessed | tf_op | source)
XLA Modules:
  0.0 59.1 jit_solution(16725200091925110387)
XLA Ops:
  0.0 0.7 %add_bitcast_fusion = f32[128]{0:T(128)S(1)} fusion(s32[1,128]{1,0:T(1,128)} %param.5), kind=kLoop, calls=%fused_computation.14 | loop fusion | flops 384 | bytes 1024 | tf_op jit(solution)/shard_map/mul | solution.py:31
  0.7 0.6 fusion.1
  1.3 0.7 %maximum_multiply_fusion.steer_ref = f32[512,128]{1,0:T(8,128)} fusion(f32[256,128]{1,0:T(8,128)S(1)} %get-tuple-element.6, f32[256,128]{1,0:T(8,128)S(1)} %get-tuple-element.5), kind=kLoop, calls=%fused_computation | loop fusion | flops 131072 | bytes 524288 | tf_op jit(solution)/shard_map/div | solution.py:32
  2.0 9.2 %gram.1.x_ref = f32[256,256]{1,0:T(8,128)} custom-call(bf16[8192,512]{1,0:T(8,128)(2,1)} %bitcast.5, s32[1,8192]{1,0:T(1,128)} %bitcast.7), custom_call_target="tpu_custom_call" | custom-call | tf_op jit(solution)/shard_map/gram/pallas_call | solution.py:69
  11.1 20.1 %all_sum.1.parts_ref = f32[8,40,256]{2,1,0:T(8,128)} custom-call(f32[256,256]{1,0:T(8,128)} %gram.1.x_ref), custom_call_target="tpu_custom_call" | custom-call | tf_op jit(solution)/shard_map/all_sum/pallas_call | solution.py:173
  31.3 18.8 %solve.1.taps_ref = bf16[256,512]{1,0:T(8,128)(2,1)} custom-call(f32[8,40,256]{2,1,0:T(8,128)} %all_sum.1.parts_ref, f32[512,128]{1,0:T(8,128)} %maximum_multiply_fusion.steer_ref), custom_call_target="tpu_custom_call" | custom-call | tf_op jit(solution)/shard_map/solve/pallas_call | solution.py:269
  50.1 9.0 %filter.1 = bf16[256,8192]{1,0:T(8,128)(2,1)} custom-call(bf16[256,512]{1,0:T(8,128)(2,1)} %solve.1.taps_ref, bf16[8192,512]{1,0:T(8,128)(2,1)} %bitcast.6), custom_call_target="tpu_custom_call" | custom-call | tf_op jit(solution)/shard_map/filter/pallas_call | solution.py:292
  (2 shorter events, 0.0 us)

commit v2 on v1

--- a/solution.py
+++ b/solution.py
@@ -304,7 +304,7 @@
 
 def per_device(snapshots, training, doppler):
     snaps = snapshots[0]
-    block = min(1024, snaps.shape[0])
+    block = min(4096, snaps.shape[0])
     packed = gram(snaps, training[None, :], block)
     parts = all_sum(packed)
     steer = steering(doppler[0], CHANNELS, PULSES)

time: 60.3 us -> 54.7 us (0.907)
  Pallas kernels: 57.1 us -> 51.9 us
    pallas_call x1, Pallas kernels: 9.03 us -> 6.15 us  [apply_taps(): pl.pallas_call(filter_kernel, grid=(cells // block,), in_specs=[pl.BlockS...]
    pallas_call x1, Pallas kernels: 9.16 us -> 6.75 us  [gram(): pl.pallas_call(functools.partial(gram_kernel, half), grid=(cells // block...]
where the time goes in v2:
time: 54.7 us; the launch traced here: 53.8 us
  Pallas kernels  51.9 us (95%)
  other arithmetic  1.97 us (4%)
    pallas_call x1, Pallas kernels, all_sum(): pl.pallas_call(functools.partial(sum_kernel, n, m), out_shape=jax.ShapeDt...  20.2 us
    pallas_call x1, Pallas kernels, solve(): pl.pallas_call(functools.partial(solve_kernel, groups), out_shape=jax.Sha...  18.8 us
    pallas_call x1, Pallas kernels, gram(): pl.pallas_call(functools.partial(gram_kernel, half), grid=(cells // block...  6.75 us
    pallas_call x1, Pallas kernels, apply_taps(): pl.pallas_call(filter_kernel, grid=(cells // block,), in_specs=[pl.BlockS...  6.15 us

profile of v2, /device:TPU:0, one launch (start us, length us, event | category | flops | bytes accessed | tf_op | source)
XLA Modules:
  0.0 53.8 jit_solution(9880492106443107611)
XLA Ops:
  0.0 0.7 %add_bitcast_fusion = f32[128]{0:T(128)S(1)} fusion(s32[1,128]{1,0:T(1,128)} %param.5), kind=kLoop, calls=%fused_computation.14 | loop fusion | flops 384 | bytes 1024 | tf_op jit(solution)/shard_map/mul | solution.py:31
  0.7 0.6 %fusion.1 = (f32[256,128]{1,0:T(8,128)S(1)}, f32[256,128]{1,0:T(8,128)S(1)}) fusion(f32[128]{0:T(128)S(1)} %add_bitcast_fusion, f32[256]{0:T(256)S(1)} %fusion.4, f32[256]{0:T(256)S(1)} %fusion.6), kind=kLoop, calls=%fused_computation.3 | loop fusion | flops 98304 | bytes 264704 | tf_op jit(solution)/shard_map/cos | solution.py:32
  1.3 0.7 %maximum_multiply_fusion.steer_ref = f32[512,128]{1,0:T(8,128)} fusion(f32[256,128]{1,0:T(8,128)S(1)} %get-tuple-element.6, f32[256,128]{1,0:T(8,128)S(1)} %get-tuple-element.5), kind=kLoop, calls=%fused_computation | loop fusion | flops 131072 | bytes 524288 | tf_op jit(solution)/shard_map/div | solution.py:32
  2.0 6.7 %gram.1.x_ref = f32[256,256]{1,0:T(8,128)} custom-call(bf16[8192,512]{1,0:T(8,128)(2,1)} %bitcast.5, s32[1,8192]{1,0:T(1,128)} %bitcast.7), custom_call_target="tpu_custom_call" | custom-call | tf_op jit(solution)/shard_map/gram/pallas_call | solution.py:69
  8.7 20.2 %all_sum.1.parts_ref = f32[8,40,256]{2,1,0:T(8,128)} custom-call(f32[256,256]{1,0:T(8,128)} %gram.1.x_ref), custom_call_target="tpu_custom_call" | custom-call | tf_op jit(solution)/shard_map/all_sum/pallas_call | solution.py:173
  28.9 18.8 %solve.1.taps_ref = bf16[256,512]{1,0:T(8,128)(2,1)} custom-call(f32[8,40,256]{2,1,0:T(8,128)} %all_sum.1.parts_ref, f32[512,128]{1,0:T(8,128)} %maximum_multiply_fusion.steer_ref), custom_call_target="tpu_custom_call" | custom-call | tf_op jit(solution)/shard_map/solve/pallas_call | solution.py:269
  47.7 6.2 %filter.1 = bf16[256,8192]{1,0:T(8,128)(2,1)} custom-call(bf16[256,512]{1,0:T(8,128)(2,1)} %solve.1.taps_ref, bf16[8192,512]{1,0:T(8,128)(2,1)} %bitcast.6), custom_call_target="tpu_custom_call" | custom-call | tf_op jit(solution)/shard_map/filter/pallas_call | solution.py:292
  (2 shorter events, 0.0 us)
